TPU v7x, 256 devices: a whole 4x4x8 slice. The times are simulated.
256 devices in a mesh: dp: 32 (over z_hi, y, core), level: 8 (over x, z_lo).
Axes of the slice: x: 4, y: 4, z: 8 (z_hi: 4, z_lo: 2; z = z_hi * 2 + z_lo), core: 2. Of those that a mesh axis runs over, the one named last changes fastest.
Arguments:
- token_ids: int32 [32, 8, 1536], P('dp', 'level'), may hold values from 0 to 1023
- decoded_mask: int32 [32, 8, 1536], P('dp', 'level'), may hold values 0 or 1
- levels_done: int32 [32], P('dp'), may hold values from 0 to 7
- code_tables: bfloat16 [8, 1024, 1024], P('level'), may hold values from -6 to 6
- mask_vectors: bfloat16 [8, 1024], P('level'), may hold values from -6 to 6
- w_qkv: bfloat16 [3, 1024, 1024], P(None, 'dp', 'level'), may hold values from -6 to 6
- w_out: bfloat16 [1024, 1024], P('level', 'dp'), may hold values from -0.1875 to 0.1875
- w_expand: bfloat16 [1024, 2048], P('dp'), may hold values from -0.1875 to 0.1875
- w_depth: bfloat16 [5, 1024], replicated, may hold values from -2.5 to 2.5
- w_project: bfloat16 [1024, 1024], P('dp'), may hold values from -0.1875 to 0.1875
- level_heads: bfloat16 [8, 1024, 1024], P('level'), may hold values from -0.1875 to 0.1875
Outputs:
- logits: bfloat16 [32, 8, 1536, 1024], P('dp', 'level')
Inputs may be any that keep to these rules, and one draw needn't show every extreme that they name: `levels_done`: levels below it are fully decoded; the level equal to it is the one being decoded.
All inputs are finite; a program needn't handle non-finite values. No bound on the sum of `decoded_mask` on one device may be relied on, other than what follows from the above.
Results may differ from a plain program's by a relative error of at most 0.006.
Values may be sent and summed in bfloat16 or wider, within the bound.
A program may use at most 128 MiB of HBM per device.

v0:
```python
import jax
import jax.numpy as jnp
from jax import lax
from jax.sharding import PartitionSpec as P

HEADS = 16


def copy_for_each(x, axis):
    copies = jnp.broadcast_to(x, (lax.axis_size(axis), *x.shape))
    return lax.all_to_all(copies, axis, split_axis=0, concat_axis=0, tiled=True)


def laid_out(tiles, dim):
    tiles = jnp.moveaxis(tiles, 0, dim)
    dims = tiles.shape
    return tiles.reshape(*dims[:dim], dims[dim] * dims[dim + 1], *dims[dim + 2 :])


def gather_directly(x, axis, dim):
    tiles = copy_for_each(x, axis)
    return laid_out(tiles, dim)


def side_by_side(arrays, axis, dim, along):
    ends, at = ([], 0)
    for a in arrays[:-1]:
        at += a.shape[along]
        ends.append(at)
    both = jnp.concatenate(arrays, axis=along)
    return tuple(jnp.split(lax.all_gather(both, axis, axis=dim, tiled=True), ends, axis=along))


def with_halo(x, sides, width):
    for axis, dim in sides:
        devices, length = (lax.axis_size(axis), x.shape[dim])
        up = [(i, (i + 1) % devices) for i in range(devices - 1)]
        down = [(j, i) for i, j in up]
        last = lax.slice_in_dim(x, length - width, length, axis=dim)
        leading = lax.slice_in_dim(x, 0, width, axis=dim)
        before = lax.ppermute(last, axis, up)
        after = lax.ppermute(leading, axis, down)
        x = jnp.concatenate([before, x, after], axis=dim)
    return x


def layer_norm(values):
    centered = values - jnp.mean(values, axis=-1, keepdims=True)
    variance = jnp.mean(centered * centered, axis=-1, keepdims=True)
    return centered * lax.rsqrt(variance + 1e-05)


def contract_with(left, shard_piece):
    return jnp.dot(left, shard_piece, preferred_element_type=jnp.float32)


def contract_three(left, shard_piece):
    return jnp.einsum("fk,jkc->jfc", left, shard_piece, preferred_element_type=jnp.float32)


def body(
    token_ids,
    decoded_mask,
    levels_done,
    code_tables,
    mask_vectors,
    w_qkv,
    w_out,
    w_expand,
    w_depth,
    w_project,
    level_heads,
):
    frames = token_ids.shape[2]
    model_width = code_tables.shape[2]
    groups = lax.axis_size("level")
    level_index = lax.axis_index("level")
    local_rows = frames // groups
    head_dim = model_width // HEADS
    scale = head_dim ** (-0.5)
    id_row = token_ids[0, 0]
    flag_row = decoded_mask[0, 0]
    done_count = levels_done[0]
    own_table = code_tables[0]
    fill_row = mask_vectors[0].astype(jnp.float32)
    all_live = level_index < done_count
    current = level_index == done_count
    use_token = all_live | current & (flag_row == 1)
    codes = lax.broadcasted_iota(jnp.int32, (frames, own_table.shape[0]), 1)
    onehot = (id_row[:, None] == codes).astype(jnp.bfloat16)
    picked = jnp.dot(onehot, own_table, preferred_element_type=jnp.float32)
    level_terms = (
        jnp.where(use_token[:, None], picked, fill_row[None, :])
        .astype(jnp.bfloat16)
        .reshape(groups, local_rows, model_width)
    )
    received = lax.all_to_all(level_terms, "level", split_axis=0, concat_axis=0, tiled=True)
    own_rows = jnp.sum(received, axis=0, dtype=jnp.float32)
    normed = layer_norm(own_rows).astype(jnp.bfloat16)
    full_columns = gather_directly(w_qkv, "level", 2)
    projected = contract_three(
        normed, lax.all_gather(full_columns, "dp", axis=1, tiled=True)
    ).astype(jnp.bfloat16)
    queries = projected[0].reshape(local_rows, HEADS, head_dim)
    running_max = jnp.full((HEADS, local_rows), -1e30, jnp.float32)
    accumulated = jnp.zeros((local_rows, HEADS, head_dim), jnp.float32)
    key_piece, value_piece = side_by_side((projected[1], projected[2]), "level", 0, 1)
    piece_rows = key_piece.shape[0]
    key_three = key_piece.reshape(piece_rows, HEADS, head_dim)
    value_three = value_piece.reshape(piece_rows, HEADS, head_dim)
    scores = (
        jnp.einsum("qhd,khd->hqk", queries, key_three, preferred_element_type=jnp.float32) * scale
    )
    new_max = jnp.maximum(running_max, jnp.max(scores, axis=-1))
    shrink = jnp.exp(running_max - new_max)
    weights = jnp.exp(scores - new_max[:, :, None])
    weight_sum = jnp.sum(weights, axis=-1)
    added = jnp.einsum(
        "hqk,khd->qhd",
        weights.astype(jnp.bfloat16),
        value_three,
        preferred_element_type=jnp.float32,
    )
    accumulated = accumulated * shrink.T[:, :, None] + added
    running_max, weight_sum, accumulated = (new_max, weight_sum, accumulated)
    attended = (
        (accumulated / weight_sum.T[:, :, None])
        .reshape(local_rows, model_width)
        .astype(jnp.bfloat16)
    )
    out_full = gather_directly(w_out, "level", 0)
    after_attn = own_rows + jnp.dot(
        attended,
        lax.all_gather(out_full, "dp", axis=1, tiled=True),
        preferred_element_type=jnp.float32,
    )
    normed_two = layer_norm(after_attn).astype(jnp.bfloat16)
    gate_linear = contract_with(normed_two, lax.all_gather(w_expand, "dp", axis=0, tiled=True))
    gated = (gate_linear[:, :model_width] * jax.nn.sigmoid(gate_linear[:, model_width:])).astype(
        jnp.bfloat16
    )
    half_width = w_depth.shape[0] // 2
    padded = with_halo(gated, (("level", 0),), half_width)
    conv = jnp.zeros((local_rows, model_width), jnp.float32)
    for tap_index in range(w_depth.shape[0]):
        conv = conv + padded[tap_index : tap_index + local_rows].astype(jnp.float32) * w_depth[
            tap_index
        ].astype(jnp.float32)
    activated = (conv * jax.nn.sigmoid(conv)).astype(jnp.bfloat16)
    after_conv = after_attn + contract_with(
        activated, lax.all_gather(w_project, "dp", axis=0, tiled=True)
    )
    final_norm = layer_norm(after_conv).astype(jnp.bfloat16)
    own_head = level_heads[0]
    logits = jnp.dot(
        lax.all_gather(final_norm, "level", axis=0, tiled=True),
        own_head,
        preferred_element_type=jnp.float32,
    ).astype(jnp.bfloat16)
    return logits[None, None]


def solution(mesh):
    return jax.shard_map(
        body,
        mesh=mesh,
        in_specs=(
            P("dp", "level", None),
            P("dp", "level", None),
            P("dp"),
            P("level", None, None),
            P("level", None),
            P(None, "dp", "level"),
            P("level", "dp"),
            P("dp", None),
            P(),
            P("dp", None),
            P("level", None, None),
        ),
        out_specs=P("dp", "level", None, None),
        check_vma=False,
    )
```

profile of v0, /device:TPU:1, one launch (start us, length us, event | category | flops | bytes accessed | tf_op | source)
XLA Modules:
  0.0 501.6 jit_solution(8657905231968769645)
XLA Ops:
  6.5 0.0 copy-start
  6.5 0.0 all-gather.7.cloned.1.call-start
  6.5 0.9 broadcast_in_dim.57
  7.5 11.9 %all_to_all.15 = bf16[8,3,32,128]{3,2,1,0:T(8,128)(2,1)S(1)} all-to-all(bf16[8,3,32,128]{3,2,1,0:T(8,128)(2,1)S(1)} %broadcast_in_dim.57), channel_id=1, replica_groups=mesh['dp'=32,'level'=8] {'level'}, dimensions={0} | all-to-all | bytes 393216 | tf_op jit(solution)/shard_map/all_to_all | solution.py:11
  19.4 0.7 copy_bitcast_fusion
  20.1 0.0 all-gather.7.cloned.1.call-update
  20.1 0.0 all-gather.9.cloned.1.call-start
  20.1 0.7 broadcast_in_dim.61
  21.5 0.7 reduce.2
  22.2 0.7 or_reduce_fusion
  22.9 0.0 copy-done
  22.9 4.3 select_convert_fusion
  27.2 60.7 %all_to_all.16 = bf16[8,192,1024]{2,1,0:T(8,128)(2,1)S(1)} all-to-all(bf16[8,192,1024]{2,1,0:T(8,128)(2,1)S(1)} %bitcast.63), channel_id=1, replica_groups=mesh['dp'=32,'level'=8] {'level'}, dimensions={0} | all-to-all | bytes 6291456 | tf_op jit(solution)/shard_map/all_to_all | solution.py:97
  87.9 1.8 convert_reduce_fusion
  89.7 0.2 multiply_reduce_fusion.3
  90.0 13.5 %all-gather.7.cloned.1.call-done = bf16[3,1024,1024]{2,1,0:T(8,128)(2,1)} async-done(((bf16[3,32,1024]{2,1,0:T(8,128)(2,1)}), bf16[3,1024,1024]{2,1,0:T(8,128)(2,1)}) %all-gather.7.cloned.1.call-update) | async-done | bytes 6291472 | tf_op jit(solution)/shard_map/all_gather | solution.py:102
  103.5 4.2 fusion.11
  107.7 0.0 copy-start.3
  107.7 0.1 fusion.46
  107.8 0.9 pad_maximum_fusion
  108.7 0.0 all-gather.9.cloned.1.call-update
  108.8 0.0 all-gather.11.cloned.1.call-start
  108.8 0.0 copy-done.3
  108.8 9.0 %all_to_all.17 = bf16[8,128,32]{1,2,0:T(8,128)(2,1)S(1)} all-to-all(bf16[8,128,32]{1,2,0:T(8,128)(2,1)S(1)} %broadcast_in_dim.59), channel_id=1, replica_groups=mesh['dp'=32,'level'=8] {'level'}, dimensions={0} | all-to-all | bytes 131072 | tf_op jit(solution)/shard_map/all_to_all | solution.py:11
  117.8 0.6 copy_bitcast_fusion.1
  118.4 0.0 all-gather.11.cloned.1.call-update
  118.5 0.0 all-gather.13.cloned.1.call-start
  118.5 0.5 all-gather.13.cloned.1.call-update
  119.1 0.0 all-gather.15.cloned.1.call-start
  119.1 0.5 all-gather.15.cloned.1.call-update
  119.6 0.0 all-gather.17.cloned.1.call-start
  119.7 0.2 copy.25
  119.9 119.0 %all-gather.9.cloned.1.call-done = bf16[1536,2048]{1,0:T(8,128)(2,1)} async-done(((bf16[192,2048]{1,0:T(8,128)(2,1)}), bf16[1536,2048]{1,0:T(8,128)(2,1)}) %all-gather.9.cloned.1.call-update) | async-done | bytes 6291472 | tf_op jit(solution)/shard_map/all_gather | solution.py:31
  238.9 6.3 %fusion.45 = (bf16[1536,1024]{1,0:T(8,128)(2,1)}, bf16[1536,1024]{1,0:T(8,128)(2,1)}) fusion(bf16[1536,2048]{1,0:T(8,128)(2,1)} %all-gather.9.cloned.1.call-done), kind=kLoop, calls=%fused_computation.81 | loop fusion | bytes 12582912 | tf_op jit(solution)/shard_map/split | solution.py:31
  245.2 4.7 copy.27
  249.9 4.7 copy.26
  254.6 11.1 %multiply_reduce_fusion = (f32[16,192]{1,0:T(8,128)S(1)}, f32[16,192,1536]{2,1,0:T(8,128)}) fusion(bf16[192,16,64]{0,2,1:T(8,128)(2,1)S(1)} %bitcast.61, bf16[1536,16,64]{0,2,1:T(8,128)(2,1)} %bitcast.60), kind=kOutput, calls=%fused_computation.1 | convolution fusion | flops 613413888 | bytes 22425600 | tf_op jit(solution)/shard_map/qhd,khd->hqk/dot_general | solution.py:112
  265.7 9.6 %fusion = f32[16,192]{1,0:T(8,128)S(1)} fusion(f32[16,192,1536]{2,1,0:T(8,128)} %get-tuple-element.22, f32[16,192]{1,0:T(8,128)S(1)} %get-tuple-element.20), kind=kLoop, calls=%fused_computation.2 | loop fusion | flops 14152704 | bytes 18898944 | tf_op jit(solution)/shard_map/reduce_sum | solution.py:117
  275.3 11.1 %divide_convert_fusion = bf16[192,16,64]{0,2,1:T(8,128)(2,1)S(1)} fusion(bf16[1536,16,64]{0,2,1:T(8,128)(2,1)} %bitcast.62, f32[16,192,1536]{2,1,0:T(8,128)} %get-tuple-element.22, f32[16,192]{1,0:T(8,128)S(1)} %get-tuple-element.20, f32[192,16]{0,1:T(8,128)S(1)} %bitcast.65, f32[192,16]{0,1:T(8,128)S(1)} %get-tuple-element.19), kind=kOutput, calls=%fused_computation.23 | convolution fusion | flops 618725376 | bytes 22450176 | tf_op jit(solution)/shard_map/hqk,khd->qhd/dot_general | solution.py:118
  286.4 11.3 %all-gather.11.cloned.1.call-done = bf16[1024,1024]{0,1:T(8,128)(2,1)} async-done(((bf16[1024,32]{0,1:T(8,128)(2,1)}), bf16[1024,1024]{0,1:T(8,128)(2,1)}) %all-gather.11.cloned.1.call-update) | async-done | bytes 2097168 | tf_op jit(solution)/shard_map/all_gather | solution.py:134
  297.7 2.5 fusion.48
  300.3 0.2 multiply_reduce_fusion.2
  300.5 0.0 copy-start.2
  300.5 57.0 %all-gather.13.cloned.1.call-done = bf16[1024,2048]{1,0:T(8,128)(2,1)} async-done(((bf16[32,2048]{1,0:T(8,128)(2,1)}), bf16[1024,2048]{1,0:T(8,128)(2,1)}) %all-gather.13.cloned.1.call-update) | async-done | bytes 4194320 | tf_op jit(solution)/shard_map/all_gather | solution.py:138
  357.5 3.2 fusion.29
  360.7 0.2 fusion.24
  360.9 1.3 collective-permute-start.1
  362.2 4.2 collective-permute-start
  366.5 0.0 copy-done.2
  366.5 46.3 %all-gather.15.cloned.1.call-done = bf16[1024,1024]{1,0:T(8,128)(2,1)} async-done(((bf16[32,1024]{1,0:T(8,128)(2,1)}), bf16[1024,1024]{1,0:T(8,128)(2,1)}) %all-gather.15.cloned.1.call-update) | async-done | bytes 2097168 | tf_op jit(solution)/shard_map/all_gather | solution.py:151
  412.8 0.0 collective-permute-done.1
  412.8 0.0 collective-permute-done
  412.8 2.7 fusion.49
  415.5 0.2 multiply_reduce_fusion.1
  415.7 0.9 multiply_convert_fusion
  416.6 0.0 all-gather.17.cloned.1.call-update
  416.7 70.3 %all-gather.17.cloned.1.call-done = bf16[1536,1024]{1,0:T(8,128)(2,1)} async-done(((bf16[192,1024]{1,0:T(8,128)(2,1)}), bf16[1536,1024]{1,0:T(8,128)(2,1)}) %all-gather.17.cloned.1.call-update) | async-done | bytes 3145744 | tf_op jit(solution)/shard_map/all_gather | solution.py:156
  487.0 0.0 copy-start.1
  487.0 7.8 %fusion.7 = bf16[1,1,1536,1024]{3,2,1,0:T(8,128)(2,1)} fusion(bf16[1536,1024]{1,0:T(8,128)(2,1)} %all-gather.17.cloned.1.call-done, bf16[1,1024,1024]{2,1,0:T(8,128)(2,1)} %param.21), kind=kOutput, calls=%fused_computation.13 | convolution fusion | flops 3222798336 | bytes 8388608 | tf_op jit(solution)/shard_map/dot_general | solution.py:155
  494.7 0.0 copy-done.1
  (10 shorter events, 0.1 us)
Async XLA Ops:
  6.5 16.4 %copy-start = (bf16[1,1024,1024]{2,1,0:T(8,128)(2,1)S(1)}, bf16[1,1024,1024]{2,1,0:T(8,128)(2,1)}, u32[]{:S(2)}) copy-start(bf16[1,1024,1024]{2,1,0:T(8,128)(2,1)} %param.14) | copy-start | bytes 6291460
  6.5 96.9 %all-gather.7.cloned.1.call-start = ((), (), s32[]{:S(2)}) async-start(), calls=%async_computation.3 | async-start | bytes 6488064 | tf_op jit(solution)/shard_map/all_gather | solution.py:102
  20.1 218.8 %all-gather.9.cloned.1.call-start = ((), (), s32[]{:S(2)}) async-start(), calls=%async_computation.4 | async-start | bytes 7077888 | tf_op jit(solution)/shard_map/all_gather | solution.py:31
  107.7 1.1 copy-start.3
  108.8 189.0 %all-gather.11.cloned.1.call-start = ((), (), s32[]{:S(2)}) async-start(), calls=%async_computation.5 | async-start | bytes 2162688 | tf_op jit(solution)/shard_map/all_gather | solution.py:134
  118.5 239.0 %all-gather.13.cloned.1.call-start = ((), (), s32[]{:S(2)}) async-start(), calls=%async_computation.6 | async-start | bytes 4325376 | tf_op jit(solution)/shard_map/all_gather | solution.py:138
  119.1 293.7 %all-gather.15.cloned.1.call-start = ((), (), s32[]{:S(2)}) async-start(), calls=%async_computation.7 | async-start | bytes 2162688 | tf_op jit(solution)/shard_map/all_gather | solution.py:151
  119.6 367.3 %all-gather.17.cloned.1.call-start = ((), (), s32[]{:S(2)}) async-start(), calls=%async_computation.8 | async-start | bytes 3538944 | tf_op jit(solution)/shard_map/all_gather | solution.py:156
  300.5 66.0 %copy-start.2 = (bf16[5,1024]{1,0:T(8,128)(2,1)S(1)}, bf16[5,1024]{1,0:T(8,128)(2,1)}, u32[]{:S(2)}) copy-start(bf16[5,1024]{1,0:T(8,128)(2,1)} %param.19) | copy-start | bytes 30724
  360.9 51.8 %collective-permute-start.1 = (bf16[2,1024]{1,0:T(2,128)(2,1)S(1)}, bf16[2,1024]{1,0:T(2,128)(2,1)S(1)}, u32[]{:S(2)}, u32[]{:S(2)}) collective-permute-start(bf16[2,1024]{1,0:T(2,128)(2,1)S(1)} %get-tuple-element.13), channel_id=1, source_target_pairs={{1,0},{2,1},{3,2},{4,3},{5,4},{6,5},{7,6},{9,8},{10,9},{11,10},{12... | collective-permute-start | bytes 12296 | tf_op jit(solution)/shard_map/ppermute | solution.py:42
  362.2 50.5 %collective-permute-start = (bf16[2,1024]{1,0:T(2,128)(2,1)S(1)}, bf16[2,1024]{1,0:T(2,128)(2,1)S(1)}, u32[]{:S(2)}, u32[]{:S(2)}) collective-permute-start(bf16[2,1024]{1,0:T(2,128)(2,1)S(1)} %get-tuple-element.12), channel_id=1, source_target_pairs={{0,1},{1,2},{2,3},{3,4},{4,5},{5,6},{6,7},{8,9},{9,10},{10,11},{11... | collective-permute-start | bytes 12296 | tf_op jit(solution)/shard_map/ppermute | solution.py:41
  487.0 7.8 %copy-start.1 = (bf16[1,1024,1024]{2,1,0:T(8,128)(2,1)S(1)}, bf16[1,1024,1024]{2,1,0:T(8,128)(2,1)}, u32[]{:S(2)}) copy-start(bf16[1,1024,1024]{2,1,0:T(8,128)(2,1)} %param.14) | copy-start | bytes 6291460
Sparse Core Ops, SparseCore 0:
  20.2 83.2 all-gather.6
  108.9 129.9 all-gather.8
  241.5 56.1 all-gather.10
  300.1 57.3 all-gather.12
  359.9 52.8 all-gather.14
  416.8 70.1 all-gather.16
where the time goes:
time: 502 us
  waiting for transfers between devices  318 us (63%)
  blocking collectives  81.6 us (16%)
  matrix products  46.9 us (9%)
  local copies, waits for them, and re-layouts  18.2 us (4%)
  other arithmetic  16.4 us (3%)
  between operations  14.3 us (3%)
  starting transfers between devices  5.7 us (1%)
    all_gather x1, waiting for transfers between devices, side_by_side(): lax.all_gather(both, axis, axis=dim, tiled=True)  119 us
    all_gather x1, waiting for transfers between devices, body(): lax.all_gather(final_norm, 'level', axis=0, tiled=True)  70.3 us
    all_to_all x1, blocking collectives, body(): lax.all_to_all(level_terms, 'level', split_axis=0, concat_axis=0, tiled=T...  60.7 us
    all_gather x1, waiting for transfers between devices, body(): lax.all_gather(w_expand, 'dp', axis=0, tiled=True)  57 us
    all_gather x1, waiting for transfers between devices, body(): lax.all_gather(w_project, 'dp', axis=0, tiled=True)  46.3 us
    all_to_all x2, blocking collectives, copy_for_each(): return lax.all_to_all(copies, axis, split_axis=0, concat_axis=0, tiled=True)  20.9 us
    split x3, local copies, waits for them, and re-layouts, side_by_side(): jnp.split(lax.all_gather(both, axis, axis=dim, tiled=True), ends, axis=al...  15.7 us
    all_gather x1, waiting for transfers between devices, body(): lax.all_gather(full_columns, 'dp', axis=1, tiled=True)  13.5 us
  transfers between devices with their start and end apart: 8, of which 6 were waited for; matrix products, arithmetic and copies ran while one was open for 13% of the time, Pallas kernels for 0%

commit v1 on v0

--- a/solution.py
+++ b/solution.py
@@ -153,7 +153,9 @@
     final_norm = layer_norm(after_conv).astype(jnp.bfloat16)
     own_head = level_heads[0]
     logits = jnp.dot(
-        lax.all_gather(final_norm, "level", axis=0, tiled=True),
+        jnp.concatenate(
+            lax.all_to_all(jnp.stack([final_norm] * lax.axis_size("level")), "level", 0, 0), axis=0
+        ),
         own_head,
         preferred_element_type=jnp.float32,
     ).astype(jnp.bfloat16)

time: 502 us -> 470 us (0.936)
  waiting for transfers between devices: 318 us -> 248 us
  blocking collectives: 81.6 us -> 123 us
    all_gather x1 -> x0, waiting for transfers between devices: 70.3 us -> none  [body(): lax.all_gather(final_norm, 'level', axis=0, tiled=True)]
    all_to_all x0 -> x1, blocking collectives: none -> 41.3 us  [body(): lax.all_to_all(jnp.stack([final_norm] * lax.axis_size('level')), 'level',...]
  transfers between devices with their start and end apart: 8 -> 7, of which waited for: 6 -> 5; matrix products, arithmetic and copies ran while one was open for 13% -> 13% of each run, Pallas kernels for 0% -> 0%
where the time goes in v1:
time: 470 us; the launch traced here: 469 us
  waiting for transfers between devices  248 us (53%)
  blocking collectives  123 us (26%)
  matrix products  43.8 us (9%)
  local copies, waits for them, and re-layouts  18.6 us (4%)
  other arithmetic  15.6 us (3%)
  between operations  14 us (3%)
  starting transfers between devices  5.66 us (1%)
    all_gather x1, waiting for transfers between devices, side_by_side(): lax.all_gather(both, axis, axis=dim, tiled=True)  119 us
    all_to_all x1, blocking collectives, body(): lax.all_to_all(level_terms, 'level', split_axis=0, concat_axis=0, tiled=T...  60.7 us
    all_gather x1, waiting for transfers between devices, body(): lax.all_gather(w_expand, 'dp', axis=0, tiled=True)  57 us
    all_gather x1, waiting for transfers between devices, body(): lax.all_gather(w_project, 'dp', axis=0, tiled=True)  46.3 us
    all_to_all x1, blocking collectives, body(): lax.all_to_all(jnp.stack([final_norm] * lax.axis_size('level')), 'level',...  41.3 us
    all_to_all x2, blocking collectives, copy_for_each(): return lax.all_to_all(copies, axis, split_axis=0, concat_axis=0, tiled=True)  20.9 us
    split x3, local copies, waits for them, and re-layouts, side_by_side(): jnp.split(lax.all_gather(both, axis, axis=dim, tiled=True), ends, axis=al...  15.7 us
    all_gather x1, waiting for transfers between devices, body(): lax.all_gather(full_columns, 'dp', axis=1, tiled=True)  13.5 us
  transfers between devices with their start and end apart: 7, of which 5 were waited for; matrix products, arithmetic and copies ran while one was open for 13% of the time, Pallas kernels for 0%

profile of v1, /device:TPU:1, one launch (start us, length us, event | category | flops | bytes accessed | tf_op | source)
XLA Modules:
  0.0 468.9 jit_solution(3161507719601360348)
XLA Ops:
  6.5 0.0 copy-start
  6.5 0.0 all-gather.6.cloned.1.call-start
  6.5 0.9 broadcast_in_dim.57
  7.5 11.9 %all_to_all.20 = bf16[8,3,32,128]{3,2,1,0:T(8,128)(2,1)S(1)} all-to-all(bf16[8,3,32,128]{3,2,1,0:T(8,128)(2,1)S(1)} %broadcast_in_dim.57), channel_id=1, replica_groups=mesh['dp'=32,'level'=8] {'level'}, dimensions={0} | all-to-all | bytes 393216 | tf_op jit(solution)/shard_map/all_to_all | solution.py:11
  19.4 0.7 copy_bitcast_fusion
  20.1 0.0 all-gather.6.cloned.1.call-update
  20.1 0.0 all-gather.8.cloned.1.call-start
  20.1 0.7 broadcast_in_dim.61
  21.5 0.7 reduce.2
  22.2 0.7 or_reduce_fusion
  22.9 0.0 copy-done
  22.9 4.3 select_convert_fusion
  27.2 60.7 %all_to_all.21 = bf16[8,192,1024]{2,1,0:T(8,128)(2,1)S(1)} all-to-all(bf16[8,192,1024]{2,1,0:T(8,128)(2,1)S(1)} %bitcast.64), channel_id=1, replica_groups=mesh['dp'=32,'level'=8] {'level'}, dimensions={0} | all-to-all | bytes 6291456 | tf_op jit(solution)/shard_map/all_to_all | solution.py:97
  87.9 1.8 convert_reduce_fusion
  89.7 0.2 multiply_reduce_fusion.3
  90.0 13.5 %all-gather.6.cloned.1.call-done = bf16[3,1024,1024]{2,1,0:T(8,128)(2,1)} async-done(((bf16[3,32,1024]{2,1,0:T(8,128)(2,1)}), bf16[3,1024,1024]{2,1,0:T(8,128)(2,1)}) %all-gather.6.cloned.1.call-update) | async-done | bytes 6291472 | tf_op jit(solution)/shard_map/all_gather | solution.py:102
  103.5 4.2 fusion.11
  107.7 0.0 copy-start.3
  107.7 0.1 fusion.46
  107.8 0.9 pad_maximum_fusion
  108.7 0.0 all-gather.8.cloned.1.call-update
  108.8 0.0 all-gather.10.cloned.1.call-start
  108.8 0.0 copy-done.3
  108.8 9.0 %all_to_all.22 = bf16[8,128,32]{1,2,0:T(8,128)(2,1)S(1)} all-to-all(bf16[8,128,32]{1,2,0:T(8,128)(2,1)S(1)} %broadcast_in_dim.59), channel_id=1, replica_groups=mesh['dp'=32,'level'=8] {'level'}, dimensions={0} | all-to-all | bytes 131072 | tf_op jit(solution)/shard_map/all_to_all | solution.py:11
  117.8 0.6 copy_bitcast_fusion.1
  118.4 0.0 all-gather.10.cloned.1.call-update
  118.5 0.0 all-gather.12.cloned.1.call-start
  118.5 0.5 all-gather.12.cloned.1.call-update
  119.0 0.0 all-gather.14.cloned.1.call-start
  119.1 0.5 all-gather.14.cloned.1.call-update
  119.6 0.2 copy.25
  119.8 119.1 %all-gather.8.cloned.1.call-done = bf16[1536,2048]{1,0:T(8,128)(2,1)} async-done(((bf16[192,2048]{1,0:T(8,128)(2,1)}), bf16[1536,2048]{1,0:T(8,128)(2,1)}) %all-gather.8.cloned.1.call-update) | async-done | bytes 6291472 | tf_op jit(solution)/shard_map/all_gather | solution.py:31
  238.9 6.3 %fusion.45 = (bf16[1536,1024]{1,0:T(8,128)(2,1)}, bf16[1536,1024]{1,0:T(8,128)(2,1)}) fusion(bf16[1536,2048]{1,0:T(8,128)(2,1)} %all-gather.8.cloned.1.call-done), kind=kLoop, calls=%fused_computation.81 | loop fusion | bytes 12582912 | tf_op jit(solution)/shard_map/split | solution.py:31
  245.2 4.7 %copy.27 = bf16[1536,1024]{0,1:T(8,128)(2,1)} copy(bf16[1536,1024]{1,0:T(8,128)(2,1)} %get-tuple-element.8) | data formatting | bytes 6291456 | tf_op jit(solution)/shard_map/split | solution.py:31
  249.9 4.6 copy.26
  254.6 11.1 %multiply_reduce_fusion = (f32[16,192]{1,0:T(8,128)S(1)}, f32[16,192,1536]{2,1,0:T(8,128)}) fusion(bf16[192,16,64]{0,2,1:T(8,128)(2,1)S(1)} %bitcast.62, bf16[1536,16,64]{0,2,1:T(8,128)(2,1)} %bitcast.61), kind=kOutput, calls=%fused_computation.1 | convolution fusion | flops 613413888 | bytes 22425600 | tf_op jit(solution)/shard_map/qhd,khd->hqk/dot_general | solution.py:112
  265.7 9.6 %fusion = f32[16,192]{1,0:T(8,128)S(1)} fusion(f32[16,192,1536]{2,1,0:T(8,128)} %get-tuple-element.22, f32[16,192]{1,0:T(8,128)S(1)} %get-tuple-element.20), kind=kLoop, calls=%fused_computation.2 | loop fusion | flops 14152704 | bytes 18898944 | tf_op jit(solution)/shard_map/reduce_sum | solution.py:117
  275.3 11.1 %divide_convert_fusion = bf16[192,16,64]{0,2,1:T(8,128)(2,1)S(1)} fusion(bf16[1536,16,64]{0,2,1:T(8,128)(2,1)} %bitcast.63, f32[16,192,1536]{2,1,0:T(8,128)} %get-tuple-element.22, f32[16,192]{1,0:T(8,128)S(1)} %get-tuple-element.20, f32[192,16]{0,1:T(8,128)S(1)} %bitcast.67, f32[192,16]{0,1:T(8,128)S(1)} %get-tuple-element.19), kind=kOutput, calls=%fused_computation.23 | convolution fusion | flops 618725376 | bytes 22450176 | tf_op jit(solution)/shard_map/hqk,khd->qhd/dot_general | solution.py:118
  286.4 11.4 %all-gather.10.cloned.1.call-done = bf16[1024,1024]{0,1:T(8,128)(2,1)} async-done(((bf16[1024,32]{0,1:T(8,128)(2,1)}), bf16[1024,1024]{0,1:T(8,128)(2,1)}) %all-gather.10.cloned.1.call-update) | async-done | bytes 2097168 | tf_op jit(solution)/shard_map/all_gather | solution.py:134
  297.7 2.5 fusion.48
  300.3 0.2 multiply_reduce_fusion.2
  300.5 0.0 copy-start.2
  300.5 57.0 %all-gather.12.cloned.1.call-done = bf16[1024,2048]{1,0:T(8,128)(2,1)} async-done(((bf16[32,2048]{1,0:T(8,128)(2,1)}), bf16[1024,2048]{1,0:T(8,128)(2,1)}) %all-gather.12.cloned.1.call-update) | async-done | bytes 4194320 | tf_op jit(solution)/shard_map/all_gather | solution.py:138
  357.5 3.2 fusion.29
  360.7 0.2 fusion.24
  360.9 1.3 collective-permute-start.1
  362.2 4.2 collective-permute-start
  366.5 0.0 copy-done.2
  366.5 46.3 %all-gather.14.cloned.1.call-done = bf16[1024,1024]{1,0:T(8,128)(2,1)} async-done(((bf16[32,1024]{1,0:T(8,128)(2,1)}), bf16[1024,1024]{1,0:T(8,128)(2,1)}) %all-gather.14.cloned.1.call-update) | async-done | bytes 2097168 | tf_op jit(solution)/shard_map/all_gather | solution.py:151
  412.8 0.0 collective-permute-done.1
  412.8 0.0 collective-permute-done
  412.8 2.7 fusion.49
  415.5 0.2 multiply_reduce_fusion.1
  415.7 0.2 multiply_convert_fusion
  415.9 0.4 stack.2
  416.3 0.0 copy-start.4
  416.3 41.3 %all_to_all.23 = bf16[8,192,1024]{2,1,0:T(8,128)(2,1)S(1)} all-to-all(bf16[8,192,1024]{2,1,0:T(8,128)(2,1)S(1)} %stack.2), channel_id=1, replica_groups=mesh['dp'=32,'level'=8] {'level'}, dimensions={0} | all-to-all | bytes 6291456 | tf_op jit(solution)/shard_map/all_to_all | solution.py:157
  457.6 0.0 copy-done.4
  457.6 0.0 copy-start.1
  457.6 4.7 %fusion.7 = bf16[1,1,1536,1024]{3,2,1,0:T(8,128)(2,1)} fusion(bf16[1536,1024]{1,0:T(8,128)(2,1)S(1)} %bitcast.65, bf16[1,1024,1024]{2,1,0:T(8,128)(2,1)S(1)} %copy-done.4), kind=kOutput, calls=%fused_computation.13 | convolution fusion | flops 3222798336 | bytes 8388608 | tf_op jit(solution)/shard_map/dot_general | solution.py:155
  462.4 0.0 copy-done.1
  (10 shorter events, 0.1 us)
Async XLA Ops:
  6.5 16.4 %copy-start = (bf16[1,1024,1024]{2,1,0:T(8,128)(2,1)S(1)}, bf16[1,1024,1024]{2,1,0:T(8,128)(2,1)}, u32[]{:S(2)}) copy-start(bf16[1,1024,1024]{2,1,0:T(8,128)(2,1)} %param.14) | copy-start | bytes 6291460
  6.5 96.9 %all-gather.6.cloned.1.call-start = ((), (), s32[]{:S(2)}) async-start(), calls=%async_computation.4 | async-start | bytes 6488064 | tf_op jit(solution)/shard_map/all_gather | solution.py:102
  20.1 218.8 %all-gather.8.cloned.1.call-start = ((), (), s32[]{:S(2)}) async-start(), calls=%async_computation.5 | async-start | bytes 7077888 | tf_op jit(solution)/shard_map/all_gather | solution.py:31
  107.7 1.1 copy-start.3
  108.8 189.0 %all-gather.10.cloned.1.call-start = ((), (), s32[]{:S(2)}) async-start(), calls=%async_computation.6 | async-start | bytes 2162688 | tf_op jit(solution)/shard_map/all_gather | solution.py:134
  118.5 239.0 %all-gather.12.cloned.1.call-start = ((), (), s32[]{:S(2)}) async-start(), calls=%async_computation.7 | async-start | bytes 4325376 | tf_op jit(solution)/shard_map/all_gather | solution.py:138
  119.0 293.7 %all-gather.14.cloned.1.call-start = ((), (), s32[]{:S(2)}) async-start(), calls=%async_computation.8 | async-start | bytes 2162688 | tf_op jit(solution)/shard_map/all_gather | solution.py:151
  300.5 66.0 %copy-start.2 = (bf16[5,1024]{1,0:T(8,128)(2,1)S(1)}, bf16[5,1024]{1,0:T(8,128)(2,1)}, u32[]{:S(2)}) copy-start(bf16[5,1024]{1,0:T(8,128)(2,1)} %param.19) | copy-start | bytes 30724
  360.9 51.8 %collective-permute-start.1 = (bf16[2,1024]{1,0:T(2,128)(2,1)S(1)}, bf16[2,1024]{1,0:T(2,128)(2,1)S(1)}, u32[]{:S(2)}, u32[]{:S(2)}) collective-permute-start(bf16[2,1024]{1,0:T(2,128)(2,1)S(1)} %get-tuple-element.13), channel_id=1, source_target_pairs={{1,0},{2,1},{3,2},{4,3},{5,4},{6,5},{7,6},{9,8},{10,9},{11,10},{12... | collective-permute-start | bytes 12296 | tf_op jit(solution)/shard_map/ppermute | solution.py:42
  362.2 50.5 %collective-permute-start = (bf16[2,1024]{1,0:T(2,128)(2,1)S(1)}, bf16[2,1024]{1,0:T(2,128)(2,1)S(1)}, u32[]{:S(2)}, u32[]{:S(2)}) collective-permute-start(bf16[2,1024]{1,0:T(2,128)(2,1)S(1)} %get-tuple-element.12), channel_id=1, source_target_pairs={{0,1},{1,2},{2,3},{3,4},{4,5},{5,6},{6,7},{8,9},{9,10},{10,11},{11... | collective-permute-start | bytes 12296 | tf_op jit(solution)/shard_map/ppermute | solution.py:41
  416.3 41.3 %copy-start.4 = (bf16[1,1024,1024]{2,1,0:T(8,128)(2,1)S(1)}, bf16[1,1024,1024]{2,1,0:T(8,128)(2,1)}, u32[]{:S(2)}) copy-start(bf16[1,1024,1024]{2,1,0:T(8,128)(2,1)} %param.21) | copy-start | bytes 6291460
  457.6 4.7 %copy-start.1 = (bf16[1,1024,1024]{2,1,0:T(8,128)(2,1)S(1)}, bf16[1,1024,1024]{2,1,0:T(8,128)(2,1)}, u32[]{:S(2)}) copy-start(bf16[1,1024,1024]{2,1,0:T(8,128)(2,1)} %param.14) | copy-start | bytes 6291460
Sparse Core Ops, SparseCore 0:
  20.2 83.2 all-gather.5
  108.9 129.9 all-gather.7
  241.5 56.2 all-gather.9
  300.1 57.2 all-gather.11
  359.9 52.8 all-gather.13
